TPU v7x, 8 devices: a whole 2x2x1 slice. The times are simulated.
8 devices in a mesh: col: 2 (over z, y), row: 4 (over x, core).
Axes of the slice: x: 2, y: 2, z: 1, core: 2. Of those that a mesh axis runs over, the one named last changes fastest.
Arguments:
- trans_mat: bfloat16 [24576, 24576], P('row', 'col')
- x_start: float32 [24576, 512], P(('col', 'row'))
- teleport: float32 [24576, 512], P(('col', 'row'))
- dangling: int32 [24576], P(('col', 'row'))
Outputs:
- output: float32 [24576, 512], P(('col', 'row'))
All inputs are finite; a program needn't handle non-finite values.
Results may differ from a plain program's by a relative error of at most 0.001.
Values are sent between devices in bfloat16 or wider.
A program may use at most 1 GiB of HBM per device.

v0:
```python
import jax
import jax.numpy as jnp
from jax import lax
from jax.sharding import PartitionSpec as P

SWEEPS = 8
DAMPING = 0.85


def solution(mesh):
    row_size = mesh.shape['row']
    col_size = mesh.shape['col']
    realign = [(col_idx * row_size + row_idx, row_idx * col_size + col_idx)
               for row_idx in range(row_size) for col_idx in range(col_size)]

    def local_sweeps(mat_tile, x_piece, tele_piece, dang_piece):
        vertex_count = mat_tile.shape[1] * col_size
        dang_col = dang_piece.astype(jnp.float32)[:, None]
        x_cur = x_piece
        for sweep_idx in range(SWEEPS):
            dang_mass = lax.psum(jnp.sum(dang_col * x_cur, axis=0), ('col', 'row')) / vertex_count
            x_src = lax.all_gather(x_cur.astype(jnp.bfloat16), 'row', axis=0, tiled=True)
            part_prod = jnp.dot(mat_tile, x_src, preferred_element_type=jnp.float32)
            folded = lax.psum_scatter(part_prod, 'col', scatter_dimension=0, tiled=True)
            aligned = lax.ppermute(folded, ('col', 'row'), perm=realign)
            x_cur = DAMPING * aligned + (DAMPING * dang_mass + (1.0 - DAMPING))[None, :] * tele_piece
        return x_cur

    vec_spec = P(('col', 'row'), None)
    return jax.shard_map(local_sweeps, mesh=mesh,
                         in_specs=(P('row', 'col'), vec_spec, vec_spec, P(('col', 'row'))),
                         out_specs=vec_spec, check_vma=False)
```

profile of v0, /device:TPU:3, one launch (start us, length us, event | category | flops | bytes accessed | tf_op | source)
XLA Modules:
  0.0 3302.3 jit_solution(8618055736305752657)
XLA Ops:
  95.0 90.1 %fusion.8 = f32[6144,512]{1,0:T(8,128)} fusion(bf16[6144,12288]{1,0:T(8,128)(2,1)} %param.4, bf16[12288,512]{1,0:T(8,128)(2,1)} %all-gather.9.cloned.1.call-done), kind=kOutput, calls=%fused_computation.39 | convolution fusion | flops 77309411328 | bytes 176160768 | tf_op jit(solution)/shard_map/dot_general | solution.py:23
  185.1 142.2 %reduce-scatter.9.cloned.1.call-done = f32[3072,512]{1,0:T(8,128)} async-done(((f32[6144,512]{1,0:T(8,128)}), f32[3072,512]{1,0:T(8,128)}) %reduce-scatter.9.cloned.1.call-update) | async-done | bytes 6291472 | tf_op jit(solution)/shard_map/reduce_scatter | solution.py:24
  330.3 86.7 %psum.56 = f32[512]{0:T(512)S(1)} all-reduce(f32[512]{0:T(512)S(1)} %get-tuple-element.20), channel_id=1, replica_groups=mesh['col'=2,'row'=4] {'col','row'}, use_global_device_ids=true, to_apply=%region_2.0 | all-reduce | flops 512 | bytes 4096 | tf_op jit(solution)/shard_map/psum | solution.py:21
  504.9 90.1 %convolution_bitcast_fusion.6 = f32[6144,512]{1,0:T(8,128)} fusion(bf16[6144,12288]{1,0:T(8,128)(2,1)} %param.4, bf16[12288,512]{1,0:T(8,128)(2,1)} %all-gather.11.cloned.1.call-done), kind=kOutput, calls=%fused_computation.6 | convolution fusion | flops 77309411328 | bytes 176160768 | tf_op jit(solution)/shard_map/dot_general | solution.py:23
  595.1 142.2 %reduce-scatter.11.cloned.1.call-done = f32[3072,512]{1,0:T(8,128)} async-done(((f32[6144,512]{1,0:T(8,128)}), f32[3072,512]{1,0:T(8,128)}) %reduce-scatter.11.cloned.1.call-update) | async-done | bytes 6291472 | tf_op jit(solution)/shard_map/reduce_scatter | solution.py:24
  740.3 86.7 %psum.57 = f32[512]{0:T(512)S(1)} all-reduce(f32[512]{0:T(512)S(1)} %get-tuple-element.18), channel_id=1, replica_groups=mesh['col'=2,'row'=4] {'col','row'}, use_global_device_ids=true, to_apply=%region_5.0 | all-reduce | flops 512 | bytes 4096 | tf_op jit(solution)/shard_map/psum | solution.py:21
  914.8 90.1 %convolution_bitcast_fusion.5 = f32[6144,512]{1,0:T(8,128)} fusion(bf16[6144,12288]{1,0:T(8,128)(2,1)} %param.4, bf16[12288,512]{1,0:T(8,128)(2,1)} %all-gather.13.cloned.1.call-done), kind=kOutput, calls=%fused_computation.5 | convolution fusion | flops 77309411328 | bytes 176160768 | tf_op jit(solution)/shard_map/dot_general | solution.py:23
  1005.0 142.2 %reduce-scatter.13.cloned.1.call-done = f32[3072,512]{1,0:T(8,128)} async-done(((f32[6144,512]{1,0:T(8,128)}), f32[3072,512]{1,0:T(8,128)}) %reduce-scatter.13.cloned.1.call-update) | async-done | bytes 6291472 | tf_op jit(solution)/shard_map/reduce_scatter | solution.py:24
  1150.2 86.7 %psum.58 = f32[512]{0:T(512)S(1)} all-reduce(f32[512]{0:T(512)S(1)} %get-tuple-element.16), channel_id=1, replica_groups=mesh['col'=2,'row'=4] {'col','row'}, use_global_device_ids=true, to_apply=%region_8.0 | all-reduce | flops 512 | bytes 4096 | tf_op jit(solution)/shard_map/psum | solution.py:21
  1324.7 90.1 %convolution_bitcast_fusion.4 = f32[6144,512]{1,0:T(8,128)} fusion(bf16[6144,12288]{1,0:T(8,128)(2,1)} %param.4, bf16[12288,512]{1,0:T(8,128)(2,1)} %all-gather.15.cloned.1.call-done), kind=kOutput, calls=%fused_computation.4 | convolution fusion | flops 77309411328 | bytes 176160768 | tf_op jit(solution)/shard_map/dot_general | solution.py:23
  1414.9 142.2 %reduce-scatter.15.cloned.1.call-done = f32[3072,512]{1,0:T(8,128)} async-done(((f32[6144,512]{1,0:T(8,128)}), f32[3072,512]{1,0:T(8,128)}) %reduce-scatter.15.cloned.1.call-update) | async-done | bytes 6291472 | tf_op jit(solution)/shard_map/reduce_scatter | solution.py:24
  1560.1 86.7 %psum.59 = f32[512]{0:T(512)S(1)} all-reduce(f32[512]{0:T(512)S(1)} %get-tuple-element.14), channel_id=1, replica_groups=mesh['col'=2,'row'=4] {'col','row'}, use_global_device_ids=true, to_apply=%region_11.0 | all-reduce | flops 512 | bytes 4096 | tf_op jit(solution)/shard_map/psum | solution.py:21
  1734.6 90.1 %convolution_bitcast_fusion.3 = f32[6144,512]{1,0:T(8,128)} fusion(bf16[6144,12288]{1,0:T(8,128)(2,1)} %param.4, bf16[12288,512]{1,0:T(8,128)(2,1)} %all-gather.17.cloned.1.call-done), kind=kOutput, calls=%fused_computation.3 | convolution fusion | flops 77309411328 | bytes 176160768 | tf_op jit(solution)/shard_map/dot_general | solution.py:23
  1824.8 142.2 %reduce-scatter.17.cloned.1.call-done = f32[3072,512]{1,0:T(8,128)} async-done(((f32[6144,512]{1,0:T(8,128)}), f32[3072,512]{1,0:T(8,128)}) %reduce-scatter.17.cloned.1.call-update) | async-done | bytes 6291472 | tf_op jit(solution)/shard_map/reduce_scatter | solution.py:24
  1970.0 86.7 %psum.60 = f32[512]{0:T(512)S(1)} all-reduce(f32[512]{0:T(512)S(1)} %get-tuple-element.12), channel_id=1, replica_groups=mesh['col'=2,'row'=4] {'col','row'}, use_global_device_ids=true, to_apply=%region_14.0 | all-reduce | flops 512 | bytes 4096 | tf_op jit(solution)/shard_map/psum | solution.py:21
  2144.5 90.1 %convolution_bitcast_fusion.2 = f32[6144,512]{1,0:T(8,128)} fusion(bf16[6144,12288]{1,0:T(8,128)(2,1)} %param.4, bf16[12288,512]{1,0:T(8,128)(2,1)} %all-gather.19.cloned.1.call-done), kind=kOutput, calls=%fused_computation.2 | convolution fusion | flops 77309411328 | bytes 176160768 | tf_op jit(solution)/shard_map/dot_general | solution.py:23
  2234.7 142.2 %reduce-scatter.19.cloned.1.call-done = f32[3072,512]{1,0:T(8,128)} async-done(((f32[6144,512]{1,0:T(8,128)}), f32[3072,512]{1,0:T(8,128)}) %reduce-scatter.19.cloned.1.call-update) | async-done | bytes 6291472 | tf_op jit(solution)/shard_map/reduce_scatter | solution.py:24
  2379.9 86.7 %psum.61 = f32[512]{0:T(512)S(1)} all-reduce(f32[512]{0:T(512)S(1)} %get-tuple-element.10), channel_id=1, replica_groups=mesh['col'=2,'row'=4] {'col','row'}, use_global_device_ids=true, to_apply=%region_17.0 | all-reduce | flops 512 | bytes 4096 | tf_op jit(solution)/shard_map/psum | solution.py:21
  2554.4 90.1 %convolution_bitcast_fusion.1 = f32[6144,512]{1,0:T(8,128)} fusion(bf16[6144,12288]{1,0:T(8,128)(2,1)} %param.4, bf16[12288,512]{1,0:T(8,128)(2,1)} %all-gather.21.cloned.1.call-done), kind=kOutput, calls=%fused_computation.1 | convolution fusion | flops 77309411328 | bytes 176160768 | tf_op jit(solution)/shard_map/dot_general | solution.py:23
  2644.6 142.2 %reduce-scatter.21.cloned.1.call-done = f32[3072,512]{1,0:T(8,128)} async-done(((f32[6144,512]{1,0:T(8,128)}), f32[3072,512]{1,0:T(8,128)}) %reduce-scatter.21.cloned.1.call-update) | async-done | bytes 6291472 | tf_op jit(solution)/shard_map/reduce_scatter | solution.py:24
  2789.8 86.7 %psum.62 = f32[512]{0:T(512)S(1)} all-reduce(f32[512]{0:T(512)S(1)} %get-tuple-element.8), channel_id=1, replica_groups=mesh['col'=2,'row'=4] {'col','row'}, use_global_device_ids=true, to_apply=%region_20.0 | all-reduce | flops 512 | bytes 4096 | tf_op jit(solution)/shard_map/psum | solution.py:21
  2964.3 90.1 %convolution_bitcast_fusion = f32[6144,512]{1,0:T(8,128)} fusion(bf16[6144,12288]{1,0:T(8,128)(2,1)} %param.4, bf16[12288,512]{1,0:T(8,128)(2,1)} %all-gather.23.cloned.1.call-done), kind=kOutput, calls=%fused_computation | convolution fusion | flops 77309411328 | bytes 176160768 | tf_op jit(solution)/shard_map/dot_general | solution.py:23
  3054.4 142.3 %reduce-scatter.23.cloned.1.call-done = f32[3072,512]{1,0:T(8,128)} async-done(((f32[6144,512]{1,0:T(8,128)}), f32[3072,512]{1,0:T(8,128)}) %reduce-scatter.23.cloned.1.call-update) | async-done | bytes 6291472 | tf_op jit(solution)/shard_map/reduce_scatter | solution.py:24
  3199.7 86.7 %psum.63 = f32[512]{0:T(512)S(1)} all-reduce(f32[512]{0:T(512)S(1)} %get-tuple-element.5), channel_id=1, replica_groups=mesh['col'=2,'row'=4] {'col','row'}, use_global_device_ids=true, to_apply=%region_23.0 | all-reduce | flops 512 | bytes 4096 | tf_op jit(solution)/shard_map/psum | solution.py:21
  (74 shorter events, 736.1 us)
Async XLA Ops:
  6.5 88.4 %all-gather.9.cloned.1.call-start = ((), (), s32[]{:S(2)}) async-start(), calls=%async_computation.8 | async-start | bytes 15728640 | tf_op jit(solution)/shard_map/all_gather | solution.py:22
  14.6 312.8 %reduce-scatter.9.cloned.1.call-start = ((), (), s32[]{:S(2)}) async-start(), calls=%async_computation.9 | async-start | bytes 18874368 | tf_op jit(solution)/shard_map/reduce_scatter | solution.py:24
  185.1 319.8 %all-gather.11.cloned.1.call-start = ((), (), s32[]{:S(2)}) async-start(), calls=%async_computation.10 | async-start | bytes 15728640 | tf_op jit(solution)/shard_map/all_gather | solution.py:22
  327.4 89.7 %collective-permute-start = (f32[3072,512]{1,0:T(8,128)}, f32[3072,512]{1,0:T(8,128)}, u32[]{:S(2)}, u32[]{:S(2)}) collective-permute-start(f32[3072,512]{1,0:T(8,128)} %reduce-scatter.9.cloned.1.call-done), channel_id=1, source_target_pairs={{0,0},{4,1},{1,2},{5,3},{2,4},{6,5},{3,6},{7,7}} | collective-permute-start | bytes 18874376 | tf_op jit(solution)/shard_map/ppermute | solution.py:25
  423.7 313.5 %reduce-scatter.11.cloned.1.call-start = ((), (), s32[]{:S(2)}) async-start(), calls=%async_computation.11 | async-start | bytes 18874368 | tf_op jit(solution)/shard_map/reduce_scatter | solution.py:24
  595.0 319.8 %all-gather.13.cloned.1.call-start = ((), (), s32[]{:S(2)}) async-start(), calls=%async_computation.12 | async-start | bytes 15728640 | tf_op jit(solution)/shard_map/all_gather | solution.py:22
  737.3 89.7 %collective-permute-start.1 = (f32[3072,512]{1,0:T(8,128)}, f32[3072,512]{1,0:T(8,128)}, u32[]{:S(2)}, u32[]{:S(2)}) collective-permute-start(f32[3072,512]{1,0:T(8,128)} %reduce-scatter.11.cloned.1.call-done), channel_id=1, source_target_pairs={{0,0},{4,1},{1,2},{5,3},{2,4},{6,5},{3,6},{7,7}} | collective-permute-start | bytes 18874376 | tf_op jit(solution)/shard_map/ppermute | solution.py:25
  833.7 313.5 %reduce-scatter.13.cloned.1.call-start = ((), (), s32[]{:S(2)}) async-start(), calls=%async_computation.13 | async-start | bytes 18874368 | tf_op jit(solution)/shard_map/reduce_scatter | solution.py:24
  1004.9 319.8 %all-gather.15.cloned.1.call-start = ((), (), s32[]{:S(2)}) async-start(), calls=%async_computation.14 | async-start | bytes 15728640 | tf_op jit(solution)/shard_map/all_gather | solution.py:22
  1147.2 89.7 %collective-permute-start.2 = (f32[3072,512]{1,0:T(8,128)}, f32[3072,512]{1,0:T(8,128)}, u32[]{:S(2)}, u32[]{:S(2)}) collective-permute-start(f32[3072,512]{1,0:T(8,128)} %reduce-scatter.13.cloned.1.call-done), channel_id=1, source_target_pairs={{0,0},{4,1},{1,2},{5,3},{2,4},{6,5},{3,6},{7,7}} | collective-permute-start | bytes 18874376 | tf_op jit(solution)/shard_map/ppermute | solution.py:25
  1243.6 313.5 %reduce-scatter.15.cloned.1.call-start = ((), (), s32[]{:S(2)}) async-start(), calls=%async_computation.15 | async-start | bytes 18874368 | tf_op jit(solution)/shard_map/reduce_scatter | solution.py:24
  1414.8 319.8 %all-gather.17.cloned.1.call-start = ((), (), s32[]{:S(2)}) async-start(), calls=%async_computation.16 | async-start | bytes 15728640 | tf_op jit(solution)/shard_map/all_gather | solution.py:22
  1557.1 89.7 %collective-permute-start.3 = (f32[3072,512]{1,0:T(8,128)}, f32[3072,512]{1,0:T(8,128)}, u32[]{:S(2)}, u32[]{:S(2)}) collective-permute-start(f32[3072,512]{1,0:T(8,128)} %reduce-scatter.15.cloned.1.call-done), channel_id=1, source_target_pairs={{0,0},{4,1},{1,2},{5,3},{2,4},{6,5},{3,6},{7,7}} | collective-permute-start | bytes 18874376 | tf_op jit(solution)/shard_map/ppermute | solution.py:25
  1653.5 313.5 %reduce-scatter.17.cloned.1.call-start = ((), (), s32[]{:S(2)}) async-start(), calls=%async_computation.17 | async-start | bytes 18874368 | tf_op jit(solution)/shard_map/reduce_scatter | solution.py:24
  1824.7 319.8 %all-gather.19.cloned.1.call-start = ((), (), s32[]{:S(2)}) async-start(), calls=%async_computation.18 | async-start | bytes 15728640 | tf_op jit(solution)/shard_map/all_gather | solution.py:22
  1967.0 89.7 %collective-permute-start.4 = (f32[3072,512]{1,0:T(8,128)}, f32[3072,512]{1,0:T(8,128)}, u32[]{:S(2)}, u32[]{:S(2)}) collective-permute-start(f32[3072,512]{1,0:T(8,128)} %reduce-scatter.17.cloned.1.call-done), channel_id=1, source_target_pairs={{0,0},{4,1},{1,2},{5,3},{2,4},{6,5},{3,6},{7,7}} | collective-permute-start | bytes 18874376 | tf_op jit(solution)/shard_map/ppermute | solution.py:25
  2063.4 313.5 %reduce-scatter.19.cloned.1.call-start = ((), (), s32[]{:S(2)}) async-start(), calls=%async_computation.19 | async-start | bytes 18874368 | tf_op jit(solution)/shard_map/reduce_scatter | solution.py:24
  2234.6 319.8 %all-gather.21.cloned.1.call-start = ((), (), s32[]{:S(2)}) async-start(), calls=%async_computation.20 | async-start | bytes 15728640 | tf_op jit(solution)/shard_map/all_gather | solution.py:22
  2376.9 89.7 %collective-permute-start.5 = (f32[3072,512]{1,0:T(8,128)}, f32[3072,512]{1,0:T(8,128)}, u32[]{:S(2)}, u32[]{:S(2)}) collective-permute-start(f32[3072,512]{1,0:T(8,128)} %reduce-scatter.19.cloned.1.call-done), channel_id=1, source_target_pairs={{0,0},{4,1},{1,2},{5,3},{2,4},{6,5},{3,6},{7,7}} | collective-permute-start | bytes 18874376 | tf_op jit(solution)/shard_map/ppermute | solution.py:25
  2473.3 313.5 %reduce-scatter.21.cloned.1.call-start = ((), (), s32[]{:S(2)}) async-start(), calls=%async_computation.21 | async-start | bytes 18874368 | tf_op jit(solution)/shard_map/reduce_scatter | solution.py:24
  2644.5 319.8 %all-gather.23.cloned.1.call-start = ((), (), s32[]{:S(2)}) async-start(), calls=%async_computation.22 | async-start | bytes 15728640 | tf_op jit(solution)/shard_map/all_gather | solution.py:22
  2786.8 89.7 %collective-permute-start.6 = (f32[3072,512]{1,0:T(8,128)}, f32[3072,512]{1,0:T(8,128)}, u32[]{:S(2)}, u32[]{:S(2)}) collective-permute-start(f32[3072,512]{1,0:T(8,128)} %reduce-scatter.21.cloned.1.call-done), channel_id=1, source_target_pairs={{0,0},{4,1},{1,2},{5,3},{2,4},{6,5},{3,6},{7,7}} | collective-permute-start | bytes 18874376 | tf_op jit(solution)/shard_map/ppermute | solution.py:25
  2883.2 313.5 %reduce-scatter.23.cloned.1.call-start = ((), (), s32[]{:S(2)}) async-start(), calls=%async_computation.23 | async-start | bytes 18874368 | tf_op jit(solution)/shard_map/reduce_scatter | solution.py:24
  3196.7 89.7 %collective-permute-start.7 = (f32[3072,512]{1,0:T(8,128)}, f32[3072,512]{1,0:T(8,128)}, u32[]{:S(2)}, u32[]{:S(2)}) collective-permute-start(f32[3072,512]{1,0:T(8,128)} %reduce-scatter.23.cloned.1.call-done), channel_id=1, source_target_pairs={{0,0},{4,1},{1,2},{5,3},{2,4},{6,5},{3,6},{7,7}} | collective-permute-start | bytes 18874376 | tf_op jit(solution)/shard_map/ppermute | solution.py:25
Sparse Core Ops, SparseCore 0:
  14.7 80.2 all-gather.8
  185.2 142.0 reduce-scatter.8
  423.9 80.9 all-gather.10
  595.1 142.0 reduce-scatter.10
  833.8 80.9 all-gather.12
  1005.1 142.0 reduce-scatter.12
  1243.7 80.9 all-gather.14
  1414.9 142.0 reduce-scatter.14
  1653.6 80.9 all-gather.16
  1824.8 142.0 reduce-scatter.16
  2063.5 80.9 all-gather.18
  2234.8 142.0 reduce-scatter.18
  2473.4 80.9 all-gather.20
  2644.6 142.0 reduce-scatter.20
  2883.3 80.9 all-gather.22
  3054.5 142.0 reduce-scatter.22
where the time goes:
time: 3340 us; the launch traced here: 3300 us
  waiting for transfers between devices  1780 us (53%)
  matrix products  721 us (22%)
  blocking collectives  694 us (21%)
  other arithmetic  63.5 us (2%)
    reduce_scatter x8, waiting for transfers between devices, local_sweeps(): folded = lax.psum_scatter(part_prod, 'col', scatter_dimension=0, tiled=True)  1140 us
    dot_general x8, matrix products, local_sweeps(): part_prod = jnp.dot(mat_tile, x_src, preferred_element_type=jnp.float32)  721 us
    psum x8, blocking collectives, local_sweeps(): lax.psum(jnp.sum(dang_col * x_cur, axis=0), ('col', 'row')) / vertex_count  694 us
    all_gather x8, waiting for transfers between devices, local_sweeps(): lax.all_gather(x_cur.astype(jnp.bfloat16), 'row', axis=0, tiled=True)  646 us
  transfers between devices with their start and end apart: 24, of which 16 were waited for; matrix products, arithmetic and copies ran while one was open for 0% of the time, Pallas kernels for 0%

commit v1 on v0

v1 whole, which is shorter than its diff:
```python
import functools

import jax
import jax.numpy as jnp
from jax import lax
from jax.experimental import pallas as pl
from jax.experimental.pallas import tpu as pltpu
from jax.sharding import PartitionSpec as P

SWEEPS = 8
DAMPING = 0.85
MESH = pl.DeviceIdType.MESH
HALVES = 2
PHASES = SWEEPS * HALVES
GROUPS = 4
CHUNKS = 3 * GROUPS
KSTEPS = 6
FIRST_FINAL = PHASES - HALVES
LIVE_GROUPS = FIRST_FINAL * GROUPS
TOTAL_GROUPS = PHASES * GROUPS


def rcopy(src, dst, send_sem, recv_sem, dev):
    return pltpu.make_async_remote_copy(src_ref=src, dst_ref=dst, send_sem=send_sem, recv_sem=recv_sem,
                                        device_id={"col": dev[0], "row": dev[1]}, device_id_type=MESH)


def kernel(a_ref, x0_ref, v_ref, w_ref, m0_ref, out_ref, vt_ref,
           xs, abuf, acc, part, recv, bst, vbuf, wbuf, mrecv, cvec, fin,
           a_sem, v_sem, w_sem, o_sem,
           fs, fr, bs, br, xsend, xrecv, csend, crecv,
           gx_s, gx_r, gc_s, gc_r, gl_s, gl_r, g_loc, vs, vr,
           ms, mr, fin_r, cred_f, cred_c, cred_x):
    col, row = lax.axis_index("col"), lax.axis_index("row")
    core = lax.rem(row, 2)
    home = col == row // 2
    far = jnp.logical_not(home)
    ydev = (1 - col, row)
    xdev = (col, lax.rem(row + 2, 4))
    cdev = (col, row + 1 - 2 * core)
    me = col * 4 + row
    n_rows, n_cols = a_ref.shape
    verts = n_cols * 2
    rows = n_rows // CHUNKS
    depth = n_cols // KSTEPS
    piece = n_rows // 2
    width = x0_ref.shape[2]
    own_base = core * n_rows

    def every_other(k):
        d = lax.rem(me + k, 8)
        return (d // 4, lax.rem(d, 4))

    barrier = pltpu.get_barrier_semaphore()
    for k in range(1, 8):
        d = every_other(k)
        pl.semaphore_signal(barrier, inc=1, device_id={"col": d[0], "row": d[1]}, device_id_type=MESH)
    pl.semaphore_wait(barrier, 7)

    def a_copy(n, kb):
        return pltpu.make_async_copy(
            a_ref.at[pl.ds(pl.multiple_of(n * rows, rows), rows),
                     pl.ds(pl.multiple_of(kb * depth, depth), depth)],
            abuf.at[kb], a_sem.at[kb])

    for kb in range(KSTEPS):
        a_copy(0, kb).start()

    def x_rows(h, r):
        return xs.at[h, pl.ds(pl.multiple_of(r * piece, piece), piece), :]

    def gather_own(h):
        return pltpu.make_async_copy(x0_ref.at[h], x_rows(h, row), g_loc.at[h])

    def gather_x(h):
        return rcopy(x0_ref.at[h], x_rows(h, row), gx_s.at[h], gx_r.at[h], xdev)

    def gather_c(h):
        return rcopy(x0_ref.at[h], x_rows(h, row), gc_s.at[h], gc_r.at[h], cdev)

    def gather_relay(h):
        r = lax.rem(row + 2, 4)
        return rcopy(x_rows(h, r), x_rows(h, r), gl_s.at[h], gl_r.at[h], cdev)

    keeper = (col, 2 * col + row // 2)
    keeps = jnp.logical_and(home, row == keeper[1])
    side = lax.rem(row, 2)

    def tele_send(h, m):
        src = v_ref.at[pl.ds(m * rows, rows), pl.ds(h * width, width)]
        dst = vt_ref.at[h, pl.ds(pl.multiple_of(side * piece + m * rows, rows), rows), :]
        return rcopy(src, dst, vs.at[h, m], vr.at[h, side * GROUPS + m + 2 * side], keeper)

    def mass_copy(slot, k):
        return rcopy(mrecv.at[slot, me], mrecv.at[slot, me], ms.at[slot], mr.at[slot], every_other(k))

    for h in range(HALVES):
        mrecv[2 + h, me] = m0_ref[h]
        for k in range(1, 8):
            mass_copy(2 + h, k).start()
    gather_x(0).start()
    gather_c(0).start()
    gather_own(0).start()

    @pl.when(jnp.logical_not(keeps))
    def _():
        for m in range(CHUNKS // 2):
            tele_send(0, m).start()

    gather_x(1).start()
    gather_c(1).start()
    gather_own(1).start()

    @pl.when(jnp.logical_not(keeps))
    def _():
        for m in range(CHUNKS // 2):
            tele_send(1, m).start()

    def gather_finish(h):
        gather_x(h).wait_recv()
        gather_relay(h).start()
        gather_own(h).wait()
        gather_c(h).wait_recv()
        gather_relay(h).wait_recv()
        gather_x(h).wait_send()
        gather_c(h).wait_send()
        gather_relay(h).wait_send()

    def own_rows(b, n):
        return xs.at[b, pl.ds(pl.multiple_of(own_base + n * rows, rows), rows), :]

    def partner_rows(b):
        return xs.at[b, pl.ds(pl.multiple_of(n_rows - own_base, n_rows), n_rows), :]

    def place(g, p):
        q = lax.div(g, GROUPS)
        n = lax.rem(g, GROUPS) * 3 + p
        return q, n, lax.rem(q + 2, 3), lax.rem(g, 2)

    def partial_send(g, p):
        slot = lax.rem(g, 2)
        return rcopy(part.at[p, slot], recv.at[p, slot], fs.at[p, slot], fr.at[p, slot], ydev)

    def back_send(g, p):
        q, n, b, slot = place(g, p)
        return rcopy(bst.at[p, slot], own_rows(b, n), bs.at[p, slot], br.at[p, slot], ydev)

    def x_send(g, p):
        q, n, b, slot = place(g, p)
        return rcopy(own_rows(b, n), own_rows(b, n), xsend.at[p], xrecv.at[lax.rem(q, 2), n], xdev)

    def c_send(g, p):
        q, n, b, slot = place(g, p)
        return rcopy(own_rows(b, n), own_rows(b, n), csend.at[p], crecv.at[b], cdev)

    def live(g):
        return jnp.logical_and(g >= 0, g < LIVE_GROUPS)

    def w_copy(n):
        return pltpu.make_async_copy(w_ref.at[pl.ds(pl.multiple_of(n * rows, rows), rows), :], wbuf, w_sem)

    def reduce_chunk(g, p):
        q, n, b, slot = place(g, p)
        x = part[p, slot] + recv[p, slot]
        w = wbuf[...]
        lanes = w.shape[1]
        wx = jnp.concatenate([x[:, k * lanes:(k + 1) * lanes] * w for k in range(width // lanes)], axis=1)
        m = jnp.sum(wx.reshape(rows // 8, 8, width), axis=0)
        ms_slot = lax.rem(q, 4)
        mrecv[ms_slot, me] = mrecv[ms_slot, me] + m
        return x.astype(jnp.bfloat16)

    def final_owner(n):
        return (row // 2, lax.rem(2 * row, 4) + lax.div(n, CHUNKS // 2))

    role = jnp.where(home, 0, 1)

    def final_send(g, p):
        q, n, b, slot = place(g, p)
        m = lax.rem(n, CHUNKS // 2)
        f = q - FIRST_FINAL
        return rcopy(part.at[p, slot], fin.at[f, role, m], fs.at[p, slot], fin_r.at[f, role, m], final_owner(n))

    def final_local(g, p):
        q, n, b, slot = place(g, p)
        o = final_owner(n)
        return jnp.logical_and(o[0] == col, o[1] == row)

    def out_copy(f, m):
        return pltpu.make_async_copy(
            fin.at[f, 0, m],
            out_ref.at[pl.ds(pl.multiple_of(m * rows, rows), rows), pl.ds(pl.multiple_of(f * width, width), width)],
            o_sem)

    src_tile = 2 * col + row // 2

    def final_reduce(f, m):
        tele = pltpu.make_async_copy(
            v_ref.at[pl.ds(pl.multiple_of(m * rows, rows), rows), pl.ds(pl.multiple_of(f * width, width), width)],
            vbuf, v_sem)
        tele.start()
        for r in range(2):
            mine = jnp.logical_and(src_tile == row, home) if r == 0 else jnp.bool_(False)

            @pl.when(jnp.logical_not(mine))
            def _():
                rcopy(fin.at[f, r, m], fin.at[f, r, m], fs.at[0, 0], fin_r.at[f, r, m], cdev).wait_recv()
        tele.wait()
        fin[f, 0, m] = (fin[f, 0, m] + fin[f, 1, m]) + cvec[f] * vbuf[...]
        out_copy(f, m).start()

    def substep(g, p):
        kind = 2 if p < 2 else 1
        q, n, _, slot = place(g, p)
        b = lax.rem(q, 3)
        h = lax.rem(q, 2)
        is_live = g < LIVE_GROUPS

        acc[...] = jnp.zeros_like(acc)
        last = jnp.logical_and(g == TOTAL_GROUPS - 1, p == 2)
        n_next = lax.rem(n + 1, CHUNKS)
        own_tele = jnp.logical_and(row == 2 * col + row // 2,
                                   lax.rem(row, 2) == lax.div(n, CHUNKS // 2))
        take_tele = jnp.logical_and(home, is_live)

        def tele_own():
            return pltpu.make_async_copy(
                v_ref.at[pl.ds(pl.multiple_of(lax.rem(n, CHUNKS // 2) * rows, rows), rows),
                         pl.ds(pl.multiple_of(h * width, width), width)], vbuf, v_sem)

        def tele_got():
            return pltpu.make_async_copy(vt_ref.at[h, pl.ds(pl.multiple_of(n * rows, rows), rows), :], vbuf, v_sem)

        @pl.when(jnp.logical_and(take_tele, own_tele))
        def _():
            tele_own().start()

        @pl.when(jnp.logical_and(take_tele, jnp.logical_not(own_tele)))
        def _():
            @pl.when(q < HALVES)
            def _():
                rcopy(vt_ref.at[h, pl.ds(pl.multiple_of(n * rows, rows), rows), :],
                      vt_ref.at[h, pl.ds(pl.multiple_of(n * rows, rows), rows), :],
                      vs.at[0, 0], vr.at[h, n], cdev).wait_recv()
            tele_got().start()

        def kstep(kb, carry):
            a_copy(n, kb).wait()
            acc[...] += jnp.dot(abuf[kb], xs[b, pl.ds(pl.multiple_of(kb * depth, depth), depth), :],
                                preferred_element_type=jnp.float32)

            @pl.when(jnp.logical_not(last))
            def _():
                a_copy(n_next, kb).start()
            return carry

        lax.fori_loop(0, KSTEPS, kstep, 0)

        if p == 2:
            @pl.when(jnp.logical_and(lax.rem(g, GROUPS) == GROUPS - 1, q < FIRST_FINAL - 1))
            def _():
                pl.semaphore_signal(cred_c, inc=1, device_id={"col": cdev[0], "row": cdev[1]}, device_id_type=MESH)

                @pl.when(far)
                def _():
                    pl.semaphore_signal(cred_x, inc=1, device_id={"col": xdev[0], "row": xdev[1]},
                                        device_id_type=MESH)

        if kind == 2:
            @pl.when(live(g - 4))
            def _():
                @pl.when(far)
                def _():
                    c_send(g - 4, p).wait_send()

            @pl.when(live(g - 3))
            def _():
                @pl.when(far)
                def _():
                    x_send(g - 3, p).wait_recv()
                    c_send(g - 3, p).start()

                @pl.when(home)
                def _():
                    x_send(g - 3, p).wait_send()
                    c_send(g - 3, p).wait_send()

            @pl.when(live(g - 2))
            def _():
                @pl.when(home)
                def _():
                    partial_send(g - 2, p).wait_send()
                    back_send(g - 2, p).wait_recv()
                    x_send(g - 2, p).start()
                    c_send(g - 2, p).start()
        else:
            @pl.when(live(g - 3))
            def _():
                @pl.when(far)
                def _():
                    c_send(g - 3, p).wait_send()

            @pl.when(live(g - 2))
            def _():
                @pl.when(far)
                def _():
                    x_send(g - 2, p).wait_recv()
                    c_send(g - 2, p).start()
                    partial_send(g - 2, p).wait_send()

                @pl.when(home)
                def _():
                    x_send(g - 2, p).wait_send()
                    c_send(g - 2, p).wait_send()

        @pl.when(g - 2 >= LIVE_GROUPS)
        def _():
            @pl.when(jnp.logical_not(final_local(g - 2, p)))
            def _():
                final_send(g - 2, p).wait_send()

        @pl.when(is_live)
        def _():
            @pl.when(home)
            def _():
                @pl.when(own_tele)
                def _():
                    tele_own().wait()

                @pl.when(jnp.logical_not(own_tele))
                def _():
                    tele_got().wait()
                part[p, slot] = DAMPING * acc[...] + cvec[h] * vbuf[...]
                if kind == 2:
                    partial_send(g, p).start()

            @pl.when(far)
            def _():
                part[p, slot] = DAMPING * acc[...]
                if kind == 1:
                    @pl.when(g >= 2)
                    def _():
                        pl.semaphore_wait(cred_f, 1)
                    partial_send(g, p).start()

        @pl.when(jnp.logical_not(is_live))
        def _():
            @pl.when(final_local(g, p))
            def _():
                fin[q - FIRST_FINAL, 0, lax.rem(n, CHUNKS // 2)] = DAMPING * acc[...]

            @pl.when(jnp.logical_not(final_local(g, p)))
            def _():
                part[p, slot] = DAMPING * acc[...]
                final_send(g, p).start()

        @pl.when(live(g - 1))
        def _():
            q1, n1, b1, slot1 = place(g - 1, p)

            @pl.when(far if kind == 2 else home)
            def _():
                w_copy(n1).start()
                partial_send(g - 1, p).wait_recv()
                w_copy(n1).wait()
                if kind == 2:
                    @pl.when(g - 3 >= 0)
                    def _():
                        back_send(g - 3, p).wait_send()
                    bst[p, slot1] = reduce_chunk(g - 1, p)
                    back_send(g - 1, p).start()
                else:
                    xs[b1, pl.ds(pl.multiple_of(own_base + n1 * rows, rows), rows), :] = reduce_chunk(g - 1, p)
                    x_send(g - 1, p).start()
                    c_send(g - 1, p).start()

                    @pl.when(g - 1 < LIVE_GROUPS - 2)
                    def _():
                        pl.semaphore_signal(cred_f, inc=1, device_id={"col": ydev[0], "row": ydev[1]},
                                            device_id_type=MESH)

    def group(g, carry):
        q, gq = lax.div(g, GROUPS), lax.rem(g, GROUPS)

        @pl.when(gq == 0)
        def _():
            @pl.when(q == 0)
            def _():
                gather_finish(0)

            @pl.when(q == 1)
            def _():
                gather_finish(1)

            @pl.when(q >= HALVES)
            def _():
                b = lax.rem(q, 3)
                rcopy(partner_rows(b), partner_rows(b), csend.at[0], crecv.at[b], cdev).wait_recv()

            slot = lax.rem(q + 2, 4)
            others = mrecv.at[slot, pl.ds(0, 7)]
            whole = rcopy(others, others, ms.at[slot], mr.at[slot], cdev)
            whole.wait_recv()
            whole.wait_send()
            mass = jnp.sum(jnp.sum(mrecv[slot], axis=0), axis=0, keepdims=True) / verts
            cvec[lax.rem(q, 2)] = DAMPING * mass + (1.0 - DAMPING)

        @pl.when(gq == 1)
        def _():
            @pl.when(jnp.logical_and(q >= 1, q - 1 < FIRST_FINAL))
            def _():
                slot = lax.rem(q - 1, 4)
                for k in range(1, 8):
                    mass_copy(slot, k).start()

            @pl.when(q < FIRST_FINAL)
            def _():
                mrecv[lax.rem(q, 4), me] = jnp.zeros((8, width), jnp.float32)

                @pl.when(q >= 1)
                def _():
                    pl.semaphore_wait(cred_c, 1)

                    @pl.when(home)
                    def _():
                        pl.semaphore_wait(cred_x, 1)

        for p in range(3):
            substep(g, p)
        return carry

    lax.fori_loop(0, TOTAL_GROUPS, group, 0)

    def finish(f):
        def body(m, carry):
            final_reduce(f, m)
            return carry
        lax.fori_loop(0, CHUNKS // 2, body, 0)

    for f in range(HALVES):
        finish(f)
    for g in (TOTAL_GROUPS - 2, TOTAL_GROUPS - 1):
        for p in range(3):
            @pl.when(jnp.logical_not(final_local(jnp.int32(g), p)))
            def _():
                final_send(jnp.int32(g), p).wait_send()
    for p in range(2):
        for g in (LIVE_GROUPS - 2, LIVE_GROUPS - 1):
            @pl.when(far)
            def _():
                back_send(jnp.int32(g), p).wait_send()

    @pl.when(jnp.logical_not(keeps))
    def _():
        for h in range(HALVES):
            for m in range(CHUNKS // 2):
                tele_send(h, m).wait_send()

    def drain(k, carry):
        out_copy(0, 0).wait()
        return carry
    lax.fori_loop(0, HALVES * (CHUNKS // 2), drain, 0)


def solution(mesh):
    def step(mat, x_piece, v_piece, dang_piece):
        i = lax.axis_index('row')
        j = lax.axis_index('col')
        n_rows, n_cols = mat.shape
        piece, vecs = x_piece.shape
        width = vecs // HALVES
        rows, depth = n_rows // CHUNKS, n_cols // KSTEPS
        lanes = min(128, width)

        dang_f = dang_piece.astype(jnp.float32)
        dang_all = lax.all_gather(dang_f, ('col', 'row'), axis=0, tiled=True)
        tile = lax.dynamic_slice(dang_all, (i * n_rows,), (n_rows,))
        weight = jnp.broadcast_to(tile[:, None], (n_rows, lanes))
        x0 = jnp.stack([x_piece[:, h * width:(h + 1) * width] for h in range(HALVES)]).astype(jnp.bfloat16)
        m0 = jnp.sum((dang_f[:, None] * x_piece).reshape(piece // 8, 8, vecs), axis=0)
        m0 = jnp.stack([m0[:, h * width:(h + 1) * width] for h in range(HALVES)])

        f32, bf16 = jnp.float32, jnp.bfloat16
        dma = pltpu.SemaphoreType.DMA
        hbm = pl.BlockSpec(memory_space=pl.ANY)
        out, _ = pl.pallas_call(
            kernel,
            out_shape=[jax.ShapeDtypeStruct((piece, vecs), f32),
                       jax.ShapeDtypeStruct((HALVES, n_rows, width), f32)],
            in_specs=[hbm, hbm, hbm, hbm, pl.BlockSpec(memory_space=pltpu.VMEM)],
            out_specs=[hbm, hbm],
            scratch_shapes=[
                pltpu.VMEM((3, n_cols, width), bf16),
                pltpu.VMEM((KSTEPS, rows, depth), bf16),
                pltpu.VMEM((rows, width), f32),
                pltpu.VMEM((3, 2, rows, width), f32),
                pltpu.VMEM((3, 2, rows, width), f32),
                pltpu.VMEM((2, 2, rows, width), bf16),
                pltpu.VMEM((rows, width), f32),
                pltpu.VMEM((rows, lanes), f32),
                pltpu.VMEM((4, 8, 8, width), f32),
                pltpu.VMEM((2, 1, width), f32),
                pltpu.VMEM((2, 2, CHUNKS // 2, rows, width), f32),
                dma((KSTEPS,)), dma, dma, dma,
                dma((3, 2)), dma((3, 2)), dma((2, 2)), dma((2, 2)),
                dma((3,)), dma((2, CHUNKS)), dma((3,)), dma((3,)),
                dma((2,)), dma((2,)), dma((2,)), dma((2,)), dma((2,)), dma((2,)), dma((2,)),
                dma((2, CHUNKS // 2)), dma((2, CHUNKS)),
                dma((4,)), dma((4,)), dma((2, 2, CHUNKS // 2)),
                pltpu.SemaphoreType.REGULAR, pltpu.SemaphoreType.REGULAR, pltpu.SemaphoreType.REGULAR,
            ],
            compiler_params=pltpu.CompilerParams(collective_id=0, has_side_effects=True,
                                                 vmem_limit_bytes=62 * 1024 * 1024),
            cost_estimate=pl.CostEstimate(flops=2 * n_rows * n_cols * vecs * SWEEPS,
                                          bytes_accessed=n_rows * n_cols * 2 * PHASES, transcendentals=0),
        )(mat, x0, v_piece, weight, m0)
        return out

    vec = P(('col', 'row'), None)
    return jax.shard_map(step, mesh=mesh, in_specs=(P('row', 'col'), vec, vec, P(('col', 'row'))),
                         out_specs=vec, check_vma=False)
```

time: 3340 us -> 1520 us (0.46); the launches traced: 3300 us -> 1520 us
  waiting for transfers between devices: 1780 us -> 0 us
  Pallas kernels: 0 us -> 1490 us
  matrix products: 721 us -> 0 us
  blocking collectives: 694 us -> 10.2 us
  other arithmetic: 63.5 us -> 7.42 us
    pallas_call x0 -> x1, Pallas kernels: none -> 1490 us  [step(): pl.pallas_call(kernel, out_shape=[jax.ShapeDtypeStruct((piece, vecs), f32...]
    reduce_scatter x8 -> x0, waiting for transfers between devices: 1140 us -> none  [local_sweeps(): folded = lax.psum_scatter(part_prod, 'col', scatter_dimension=0, tiled=True)]
    dot_general x8 -> x0, matrix products: 721 us -> none  [local_sweeps(): part_prod = jnp.dot(mat_tile, x_src, preferred_element_type=jnp.float32)]
    psum x8 -> x0, blocking collectives: 694 us -> none  [local_sweeps(): lax.psum(jnp.sum(dang_col * x_cur, axis=0), ('col', 'row')) / vertex_count]
    all_gather x8 -> x0, waiting for transfers between devices: 646 us -> none  [local_sweeps(): lax.all_gather(x_cur.astype(jnp.bfloat16), 'row', axis=0, tiled=True)]
    convert_element_type x8 -> x1, other arithmetic: 47.9 us -> 0.71 us  [step(): dang_f = dang_piece.astype(jnp.float32)]
  transfers between devices with their start and end apart: 24 -> 0, of which waited for: 16 -> 0; matrix products, arithmetic and copies ran while one was open for 0% -> 0% of each run, Pallas kernels for 0% -> 0%
where the time goes in v1:
time: 1520 us
  Pallas kernels  1490 us (98%)
    pallas_call x1, Pallas kernels, step(): pl.pallas_call(kernel, out_shape=[jax.ShapeDtypeStruct((piece, vecs), f32...  1490 us

profile of v1, /device:TPU:3, one launch (start us, length us, event | category | flops | bytes accessed | tf_op | source)
XLA Modules:
  0.0 1519.6 jit_solution(5563049763654344591)
XLA Ops:
  0.0 0.7 convert_element_type.4
  0.7 0.0 copy-start
  0.7 3.8 bitcast_reduce_fusion
  4.5 0.6 pad_maximum_fusion.1.m0_ref
  5.1 10.2 all_gather.3
  15.3 2.2 broadcast_in_dim.2.w_ref
  17.5 0.0 copy-done
  17.5 0.4 convert.8
  17.9 0.2 slice_bitcast_fusion.1
  18.1 1.9 pad_maximum_fusion.x0_ref
  20.1 1493.4 %shard_map.46 = (f32[3072,512]{1,0:T(8,128)}, f32[2,6144,256]{2,1,0:T(8,128)}) custom-call(bf16[6144,12288]{1,0:T(8,128)(2,1)} %a_ref.1, bf16[2,3072,256]{2,1,0:T(8,128)(2,1)} %pad_maximum_fusion.x0_ref, f32[3072,512]{1,0:T(8,128)} %v_ref.1, f32[6144,128]{1,0:T(8,128)} %broadcast_in_dim.2.w_ref, f32[2,8,256]{2,1,0:T(8,128)} %pad_maximum_fusion.1.m0_ref), custom_call_target="tpu_custom_call" | custom-call | flops 618475290624 | bytes 2415919104 | tf_op jit(solution)/shard_map/pallas_call | solution.py:486
  1513.4 6.2 copy.6
  (2 shorter events, 0.0 us)
Async XLA Ops:
  0.7 16.8 %copy-start = (f32[3072,512]{1,0:T(8,128)S(1)}, f32[3072,512]{1,0:T(8,128)}, u32[]{:S(2)}) copy-start(f32[3072,512]{1,0:T(8,128)} %param.5) | copy-start | bytes 18874372

commit v2 on v0

v2 whole, which is shorter than its diff:
```python
import jax
import jax.numpy as jnp
from jax import lax
from jax.experimental import pallas as pl
from jax.experimental.pallas import tpu as pltpu
from jax.sharding import PartitionSpec as P

SWEEPS = 8
DAMPING = 0.85
MESH = pl.DeviceIdType.MESH
HALVES = 2
PHASES = SWEEPS * HALVES
GROUPS = 3
CHUNKS = 4 * GROUPS
PIECE_CHUNKS = CHUNKS // 2
KSTEPS = 6
UNITS = (7, 9, 7, 9)
FIRST_FINAL = PHASES - HALVES
LIVE_GROUPS = FIRST_FINAL * GROUPS
TOTAL_GROUPS = PHASES * GROUPS


def rcopy(src, dst, send_sem, recv_sem, dev):
    return pltpu.make_async_remote_copy(src_ref=src, dst_ref=dst, send_sem=send_sem, recv_sem=recv_sem,
                                        device_id={"col": dev[0], "row": dev[1]}, device_id_type=MESH)


def signal(sem, dev):
    pl.semaphore_signal(sem, inc=1, device_id={"col": dev[0], "row": dev[1]}, device_id_type=MESH)


def kernel(a_ref, x0_ref, v_ref, w_ref, m0_ref, out_ref, vt_ref,
           xs, abuf, acc, part0, part1, part2, part3, recv0, recv1, recv3, side_in, cross_in, bst, round_in,
           vbuf, wbuf, mrecv, cvec, fin,
           a_sem, v_sem, w_sem, o_sem,
           fs, fr, side_r, cross_s, cross_r, bs, round_r, round_s, yrecv, xsend, xrecv, csend, crecv,
           gx_s, gx_r, gc_s, gc_r, gl_s, gl_r, g_loc, vs, vr,
           ms, mr, fin_r, cred_f, cred_side, cred_cross, cred_round, cred_c, cred_x, cred_y):
    col, row = lax.axis_index("col"), lax.axis_index("row")
    core = lax.rem(row, 2)
    home = col == row // 2
    far = jnp.logical_not(home)
    ydev = (1 - col, row)
    xdev = (col, lax.rem(row + 2, 4))
    cdev = (col, row + 1 - 2 * core)
    me = col * 4 + row
    n_rows, n_cols = a_ref.shape
    verts = n_cols * 2
    unit = n_rows // 96
    size = tuple(u * unit for u in UNITS)
    start = (0, size[0], size[0] + size[1], size[0] + size[1] + size[2])
    span = sum(size)
    depth = n_cols // KSTEPS
    piece = n_rows // 2
    width = x0_ref.shape[2]
    own_base = core * n_rows
    parts = (part0, part1, part2, part3)
    recvs = (recv0, recv1, None, recv3)

    def every_other(k):
        d = lax.rem(me + k, 8)
        return (d // 4, lax.rem(d, 4))

    barrier = pltpu.get_barrier_semaphore()
    for k in range(1, 8):
        signal(barrier, every_other(k))
    pl.semaphore_wait(barrier, 7)

    def tile_rows(gq, p):
        return pl.ds(pl.multiple_of(gq * span + start[p], unit), size[p])

    def half_cols(h):
        return pl.ds(pl.multiple_of(h * width, width), width)

    def a_copy(gq, p, kb):
        return pltpu.make_async_copy(
            a_ref.at[tile_rows(gq, p), pl.ds(pl.multiple_of(kb * depth, depth), depth)],
            abuf.at[kb, pl.ds(0, size[p])], a_sem.at[kb])

    for kb in range(KSTEPS):
        a_copy(0, 0, kb).start()

    def x_rows(h, r):
        return xs.at[h, pl.ds(pl.multiple_of(r * piece, piece), piece), :]

    def gather_own(h):
        return pltpu.make_async_copy(x0_ref.at[h], x_rows(h, row), g_loc.at[h])

    def gather_x(h):
        return rcopy(x0_ref.at[h], x_rows(h, row), gx_s.at[h], gx_r.at[h], xdev)

    def gather_c(h):
        return rcopy(x0_ref.at[h], x_rows(h, row), gc_s.at[h], gc_r.at[h], cdev)

    def gather_relay(h):
        r = lax.rem(row + 2, 4)
        return rcopy(x_rows(h, r), x_rows(h, r), gl_s.at[h], gl_r.at[h], cdev)

    keeper = (col, 2 * col + row // 2)
    keeps = jnp.logical_and(home, row == keeper[1])

    def piece_start(m):
        return (m // 2) * (size[0] + size[1]) + (m % 2) * size[0]

    def tele_send(h, m):
        rows = size[m % 2]
        src = v_ref.at[pl.ds(piece_start(m), rows), pl.ds(h * width, width)]
        dst = vt_ref.at[h, pl.ds(pl.multiple_of(core * piece + piece_start(m), unit), rows), :]
        return rcopy(src, dst, vs.at[h, m], vr.at[h, core * PIECE_CHUNKS + m], keeper)

    def mass_copy(slot, k):
        return rcopy(mrecv.at[slot, me], mrecv.at[slot, me], ms.at[slot], mr.at[slot], every_other(k))

    for h in range(HALVES):
        mrecv[2 + h, me] = m0_ref[h]
        for k in range(1, 8):
            mass_copy(2 + h, k).start()

    for h in range(HALVES):
        gather_x(h).start()
        gather_c(h).start()
        gather_own(h).start()

        @pl.when(jnp.logical_not(keeps))
        def _():
            for m in range(PIECE_CHUNKS):
                tele_send(h, m).start()

    def gather_finish(h):
        gather_x(h).wait_recv()
        gather_relay(h).start()
        gather_own(h).wait()
        gather_c(h).wait_recv()
        gather_relay(h).wait_recv()
        gather_x(h).wait_send()
        gather_c(h).wait_send()
        gather_relay(h).wait_send()

    def live(g):
        return jnp.logical_and(g >= 0, g < LIVE_GROUPS)

    def own_rows(g, p):
        b = lax.rem(lax.div(g, GROUPS) + 2, 3)
        gq = lax.rem(g, GROUPS)
        return xs.at[b, pl.ds(pl.multiple_of(own_base + gq * span + start[p], unit), size[p]), :]

    def chunk_of(g, p):
        return lax.rem(g, GROUPS) * 4 + p

    def parity(g):
        return lax.rem(lax.div(g, GROUPS), 2)

    def f_send(g, p):
        slot = lax.rem(g, 2)
        return rcopy(parts[p].at[slot], recvs[p].at[slot], fs.at[p, slot], fr.at[p, slot], ydev)

    def side_send(g):
        slot, in_slot = lax.rem(g, 2), lax.rem(g, 3)
        return rcopy(part2.at[slot], side_in.at[in_slot], fs.at[2, slot], side_r.at[in_slot], xdev)

    def cross_send(g):
        slot, in_slot = lax.rem(g, 2), lax.rem(g, 3)
        return rcopy(side_in.at[in_slot], cross_in.at[slot], cross_s, cross_r.at[slot], ydev)

    def round_send(g):
        slot, in_slot = lax.rem(g, 2), lax.rem(g, 4)
        return rcopy(bst.at[slot], round_in.at[in_slot], bs.at[slot], round_r.at[in_slot], xdev)

    def round_pass(g):
        in_slot = lax.rem(g, 4)
        return rcopy(round_in.at[in_slot], own_rows(g, 0), round_s, yrecv.at[parity(g), lax.rem(g, GROUPS)], ydev)

    def x_send(g, p):
        return rcopy(own_rows(g, p), own_rows(g, p), xsend.at[p], xrecv.at[parity(g), chunk_of(g, p)], xdev)

    def c_send(g, p):
        b = lax.rem(lax.div(g, GROUPS) + 2, 3)
        return rcopy(own_rows(g, p), own_rows(g, p), csend.at[p], crecv.at[b], cdev)

    def w_copy(which, g, p):
        return pltpu.make_async_copy(w_ref.at[which, tile_rows(lax.rem(g, GROUPS), p), :],
                                     wbuf.at[pl.ds(0, size[p])], w_sem)

    def new_rows(g, p, one, two):
        x = one + two
        w = wbuf[0:size[p]]
        lanes = w.shape[1]
        wx = jnp.concatenate([x[:, k * lanes:(k + 1) * lanes] * w for k in range(width // lanes)], axis=1)
        slot = lax.rem(lax.div(g, GROUPS), 4)
        mrecv[slot, me] = mrecv[slot, me] + jnp.sum(wx.reshape(size[p] // 8, 8, width), axis=0)
        return x.astype(jnp.bfloat16)

    def put_rows(g, p, value):
        b = lax.rem(lax.div(g, GROUPS) + 2, 3)
        gq = lax.rem(g, GROUPS)
        xs[b, pl.ds(pl.multiple_of(own_base + gq * span + start[p], unit), size[p]), :] = value

    def share(g, p):
        x_send(g, p).start()
        c_send(g, p).start()

    def sent(g, p, role, both):
        @pl.when(jnp.logical_and(live(g), role))
        def _():
            if both:
                x_send(g, p).wait_send()
            c_send(g, p).wait_send()

    def take_side(g, p, role):
        sent(g - 1, p, role, False)

        @pl.when(jnp.logical_and(live(g), role))
        def _():
            x_send(g, p).wait_recv()
            c_send(g, p).start()

    def credit(sem, dev, g, depth_):
        @pl.when(g < LIVE_GROUPS - depth_)
        def _():
            signal(sem, dev)

    def need(sem, g, depth_):
        @pl.when(g >= depth_)
        def _():
            pl.semaphore_wait(sem, 1)

    def home_reduce(g, p):
        sent(g - 1, p, home, True)

        @pl.when(jnp.logical_and(live(g), home))
        def _():
            slot = lax.rem(g, 2)
            f_send(g, p).wait_recv()
            w_copy(0, g, p).wait()
            put_rows(g, p, new_rows(g, p, parts[p][slot], recvs[p][slot]))
            share(g, p)
            credit(cred_f.at[p], ydev, g, 2)

    def far_reduce(g):
        @pl.when(jnp.logical_and(live(g), far))
        def _():
            slot = lax.rem(g, 2)
            f_send(g, 0).wait_recv()
            w_copy(0, g, 0).wait()

            @pl.when(g >= 2)
            def _():
                round_send(g - 2).wait_send()
            bst[slot] = new_rows(g, 0, part0[slot], recv0[slot])
            need(cred_round, g, 4)
            round_send(g).start()
            credit(cred_f.at[0], ydev, g, 2)

    def round_relay(g):
        @pl.when(jnp.logical_and(live(g - 1), home))
        def _():
            round_pass(g - 1).wait_send()
            credit(cred_round, xdev, g - 1, 4)

        @pl.when(jnp.logical_and(live(g), home))
        def _():
            round_send(g).wait_recv()
            round_pass(g).start()

    def round_take(g):
        sent(g - 1, 0, far, True)

        @pl.when(jnp.logical_and(live(g), far))
        def _():
            round_pass(g).wait_recv()
            share(g, 0)

    def cross_relay(g):
        @pl.when(jnp.logical_and(live(g - 1), home))
        def _():
            cross_send(g - 1).wait_send()
            credit(cred_side, xdev, g - 1, 3)

        @pl.when(jnp.logical_and(live(g), home))
        def _():
            side_send(g).wait_recv()
            need(cred_cross, g, 2)
            cross_send(g).start()

    def cross_reduce(g):
        sent(g - 1, 2, far, True)

        @pl.when(jnp.logical_and(live(g), far))
        def _():
            side_send(g).wait_recv()
            cross_send(g).wait_recv()
            w_copy(1, g, 2).wait()
            put_rows(g, 2, new_rows(g, 2, side_in[lax.rem(g, 3)], cross_in[lax.rem(g, 2)]))
            share(g, 2)
            credit(cred_side, xdev, g, 3)
            credit(cred_cross, ydev, g, 2)

    role = jnp.where(home, 0, 1)

    def final_place(g, p):
        n = chunk_of(g, p)
        side = lax.div(n, PIECE_CHUNKS)
        f = lax.div(g, GROUPS) - FIRST_FINAL
        at = lax.rem(g, GROUPS) * span + start[p] - side * piece
        return f, lax.rem(n, PIECE_CHUNKS), pl.ds(pl.multiple_of(at, unit), size[p]), (row // 2, lax.rem(2 * row, 4) + side)

    def final_send(g, p):
        f, m, rows, owner = final_place(g, p)
        slot = lax.rem(g, 2)
        return rcopy(parts[p].at[slot], fin.at[f, role, rows], fs.at[p, slot], fin_r.at[f, role, m], owner)

    def final_local(g, p):
        owner = final_place(g, p)[3]
        return jnp.logical_and(owner[0] == col, owner[1] == row)

    def fin_rows(j, k):
        return pl.ds(pl.multiple_of(j * (size[0] + size[1]) + k * size[0], unit), size[k])

    def out_copy(f, j, k):
        return pltpu.make_async_copy(fin.at[f, 0, fin_rows(j, k)],
                                     out_ref.at[fin_rows(j, k), half_cols(f)], o_sem)

    own_tile = 2 * col + row // 2 == row

    def final_reduce(f, j, k):
        rows = fin_rows(j, k)
        tele = pltpu.make_async_copy(v_ref.at[rows, half_cols(f)], vbuf.at[pl.ds(0, size[k])], v_sem)
        tele.start()
        for r in range(2):
            skip = jnp.logical_and(own_tile, home) if r == 0 else jnp.bool_(False)

            @pl.when(jnp.logical_not(skip))
            def _():
                rcopy(fin.at[f, r, rows], fin.at[f, r, rows], fs.at[0, 0], fin_r.at[f, r, 2 * j + k], cdev).wait_recv()
        tele.wait()
        fin[f, 0, rows] = (fin[f, 0, rows] + fin[f, 1, rows]) + cvec[f] * vbuf[0:size[k]]
        out_copy(f, j, k).start()

    def substep(g, p):
        q, gq = lax.div(g, GROUPS), lax.rem(g, GROUPS)
        n = gq * 4 + p
        b, h, slot = lax.rem(q, 3), lax.rem(q, 2), lax.rem(g, 2)
        rows = size[p]
        is_live = g < LIVE_GROUPS
        side = lax.div(n, PIECE_CHUNKS)
        own_tele = jnp.logical_and(own_tile, core == side)
        take_tele = jnp.logical_and(home, is_live)

        def tele_own():
            at = gq * span + start[p] - side * piece
            return pltpu.make_async_copy(v_ref.at[pl.ds(pl.multiple_of(at, unit), rows), half_cols(h)],
                                         vbuf.at[pl.ds(0, rows)], v_sem)

        def tele_got():
            return pltpu.make_async_copy(vt_ref.at[h, tile_rows(gq, p), :], vbuf.at[pl.ds(0, rows)], v_sem)

        @pl.when(jnp.logical_and(take_tele, own_tele))
        def _():
            tele_own().start()

        @pl.when(jnp.logical_and(take_tele, jnp.logical_not(own_tele)))
        def _():
            @pl.when(q < HALVES)
            def _():
                got = vt_ref.at[h, tile_rows(gq, p), :]
                rcopy(got, got, vs.at[0, 0], vr.at[h, n], cdev).wait_recv()
            tele_got().start()

        if p in (1, 3):
            @pl.when(jnp.logical_and(live(g - 1), home))
            def _():
                w_copy(0, g - 1, p).start()
        if p == 0:
            @pl.when(jnp.logical_and(live(g - 1), far))
            def _():
                w_copy(0, g - 1, 0).start()
        if p == 1:
            @pl.when(jnp.logical_and(live(g - 2), far))
            def _():
                w_copy(1, g - 2, 2).start()

        acc[0:rows] = jnp.zeros((rows, width), jnp.float32)
        nxt_p = (p + 1) % 4
        nxt_gq = lax.rem(gq + 1, GROUPS) if p == 3 else gq
        more = g < TOTAL_GROUPS - 1 if p == 3 else jnp.bool_(True)

        def kstep(kb, carry):
            a_copy(gq, p, kb).wait()
            acc[0:rows] += jnp.dot(abuf[kb, 0:rows], xs[b, pl.ds(pl.multiple_of(kb * depth, depth), depth), :],
                                   preferred_element_type=jnp.float32)

            @pl.when(more)
            def _():
                a_copy(nxt_gq, nxt_p, kb).start()
            return carry

        lax.fori_loop(0, KSTEPS, kstep, 0)

        if p == 3:
            @pl.when(jnp.logical_and(gq == GROUPS - 1, q < FIRST_FINAL - 1))
            def _():
                signal(cred_c, cdev)

                @pl.when(far)
                def _():
                    signal(cred_x, xdev)
                    signal(cred_y, ydev)

        sender = {0: home, 1: far, 2: jnp.bool_(True), 3: far}[p]

        @pl.when(jnp.logical_and(live(g - 2), sender))
        def _():
            (side_send(g - 2) if p == 2 else f_send(g - 2, p)).wait_send()

        @pl.when(g - 2 >= LIVE_GROUPS)
        def _():
            @pl.when(jnp.logical_not(final_local(g - 2, p)))
            def _():
                final_send(g - 2, p).wait_send()

        @pl.when(is_live)
        def _():
            @pl.when(home)
            def _():
                @pl.when(own_tele)
                def _():
                    tele_own().wait()

                @pl.when(jnp.logical_not(own_tele))
                def _():
                    tele_got().wait()
                parts[p][slot] = DAMPING * acc[0:rows] + cvec[h] * vbuf[0:rows]

            @pl.when(far)
            def _():
                parts[p][slot] = DAMPING * acc[0:rows]

            if p == 2:
                need(cred_side, g, 3)
                side_send(g).start()
            else:
                @pl.when(sender)
                def _():
                    need(cred_f.at[p], g, 2)
                    f_send(g, p).start()

        @pl.when(jnp.logical_not(is_live))
        def _():
            f, m, at, owner = final_place(g, p)

            @pl.when(final_local(g, p))
            def _():
                fin[f, 0, at] = DAMPING * acc[0:rows]

            @pl.when(jnp.logical_not(final_local(g, p)))
            def _():
                parts[p][slot] = DAMPING * acc[0:rows]
                final_send(g, p).start()

        if p == 0:
            take_side(g - 3, 2, home)
            take_side(g - 2, 1, far)
            far_reduce(g - 1)
        if p == 1:
            take_side(g - 3, 0, home)
            cross_reduce(g - 2)
            home_reduce(g - 1, 1)
        if p == 2:
            round_take(g - 2)
            take_side(g - 2, 3, far)
            cross_relay(g - 1)
        if p == 3:
            round_relay(g - 1)
            home_reduce(g - 1, 3)

    def group(g, carry):
        q, gq = lax.div(g, GROUPS), lax.rem(g, GROUPS)

        @pl.when(gq == 0)
        def _():
            @pl.when(q == 0)
            def _():
                gather_finish(0)

            @pl.when(q == 1)
            def _():
                gather_finish(1)

            @pl.when(q >= HALVES)
            def _():
                other = xs.at[lax.rem(q, 3), pl.ds(pl.multiple_of(n_rows - own_base, n_rows), n_rows), :]
                rcopy(other, other, csend.at[0], crecv.at[lax.rem(q, 3)], cdev).wait_recv()

            slot = lax.rem(q + 2, 4)
            others = mrecv.at[slot, pl.ds(0, 7)]
            whole = rcopy(others, others, ms.at[slot], mr.at[slot], cdev)
            whole.wait_recv()
            whole.wait_send()
            mass = jnp.sum(jnp.sum(mrecv[slot], axis=0), axis=0, keepdims=True) / verts
            cvec[lax.rem(q, 2)] = DAMPING * mass + (1.0 - DAMPING)

            @pl.when(q < FIRST_FINAL)
            def _():
                mrecv[lax.rem(q, 4), me] = jnp.zeros((8, width), jnp.float32)

        @pl.when(jnp.logical_and(gq == 1, jnp.logical_and(q >= 1, q < FIRST_FINAL)))
        def _():
            pl.semaphore_wait(cred_c, 1)

            @pl.when(home)
            def _():
                pl.semaphore_wait(cred_x, 1)
                pl.semaphore_wait(cred_y, 1)

        @pl.when(jnp.logical_and(gq == 2, jnp.logical_and(q >= 1, q - 1 < FIRST_FINAL)))
        def _():
            for k in range(1, 8):
                mass_copy(lax.rem(q - 1, 4), k).start()

        for p in range(4):
            substep(g, p)
        return carry

    lax.fori_loop(0, TOTAL_GROUPS, group, 0)

    for f in range(HALVES):
        def body(j, carry):
            final_reduce(f, j, 0)
            final_reduce(f, j, 1)
            return carry
        lax.fori_loop(0, PIECE_CHUNKS // 2, body, 0)

    for g in (TOTAL_GROUPS - 2, TOTAL_GROUPS - 1):
        for p in range(4):
            @pl.when(jnp.logical_not(final_local(jnp.int32(g), p)))
            def _():
                final_send(jnp.int32(g), p).wait_send()

    @pl.when(far)
    def _():
        for g in (LIVE_GROUPS - 2, LIVE_GROUPS - 1):
            round_send(jnp.int32(g)).wait_send()

    @pl.when(jnp.logical_not(keeps))
    def _():
        for h in range(HALVES):
            for m in range(PIECE_CHUNKS):
                tele_send(h, m).wait_send()

    def drain(j, carry):
        out_copy(0, 0, 0).wait()
        out_copy(0, 0, 1).wait()
        return carry
    lax.fori_loop(0, HALVES * PIECE_CHUNKS // 2, drain, 0)


def solution(mesh):
    def step(mat, x_piece, v_piece, dang_piece):
        i = lax.axis_index('row')
        n_rows, n_cols = mat.shape
        piece, vecs = x_piece.shape
        width = vecs // HALVES
        unit, depth = n_rows // 96, n_cols // KSTEPS
        small, large = UNITS[0] * unit, UNITS[1] * unit
        lanes = min(128, width)

        dang_f = dang_piece.astype(jnp.float32)
        dang_all = lax.all_gather(dang_f, ('col', 'row'), axis=0, tiled=True)
        tiles = jnp.stack([lax.dynamic_slice(dang_all, (i * n_rows,), (n_rows,)),
                           lax.dynamic_slice(dang_all, (lax.rem(i + 2, 4) * n_rows,), (n_rows,))])
        weight = jnp.broadcast_to(tiles[:, :, None], (2, n_rows, lanes))
        x0 = jnp.stack([x_piece[:, h * width:(h + 1) * width] for h in range(HALVES)]).astype(jnp.bfloat16)
        m0 = jnp.sum((dang_f[:, None] * x_piece).reshape(piece // 8, 8, vecs), axis=0)
        m0 = jnp.stack([m0[:, h * width:(h + 1) * width] for h in range(HALVES)])

        f32, bf16 = jnp.float32, jnp.bfloat16
        dma, regular = pltpu.SemaphoreType.DMA, pltpu.SemaphoreType.REGULAR
        hbm = pl.BlockSpec(memory_space=pl.ANY)
        out, _ = pl.pallas_call(
            kernel,
            out_shape=[jax.ShapeDtypeStruct((piece, vecs), f32),
                       jax.ShapeDtypeStruct((HALVES, n_rows, width), f32)],
            in_specs=[hbm, hbm, hbm, hbm, pl.BlockSpec(memory_space=pltpu.VMEM)],
            out_specs=[hbm, hbm],
            scratch_shapes=[
                pltpu.VMEM((3, n_cols, width), bf16),
                pltpu.VMEM((KSTEPS, large, depth), bf16),
                pltpu.VMEM((large, width), f32),
                pltpu.VMEM((2, small, width), f32),
                pltpu.VMEM((2, large, width), f32),
                pltpu.VMEM((2, small, width), f32),
                pltpu.VMEM((2, large, width), f32),
                pltpu.VMEM((2, small, width), f32),
                pltpu.VMEM((2, large, width), f32),
                pltpu.VMEM((2, large, width), f32),
                pltpu.VMEM((3, small, width), f32),
                pltpu.VMEM((2, small, width), f32),
                pltpu.VMEM((2, small, width), bf16),
                pltpu.VMEM((4, small, width), bf16),
                pltpu.VMEM((large, width), f32),
                pltpu.VMEM((large, lanes), f32),
                pltpu.VMEM((4, 8, 8, width), f32),
                pltpu.VMEM((2, 1, width), f32),
                pltpu.VMEM((2, 2, piece, width), f32),
                dma((KSTEPS,)), dma, dma, dma,
                dma((4, 2)), dma((4, 2)),
                dma((3,)), dma, dma((2,)),
                dma((2,)), dma((4,)), dma, dma((2, GROUPS)),
                dma((4,)), dma((2, CHUNKS)), dma((4,)), dma((3,)),
                dma((2,)), dma((2,)), dma((2,)), dma((2,)), dma((2,)), dma((2,)), dma((2,)),
                dma((2, PIECE_CHUNKS)), dma((2, CHUNKS)),
                dma((4,)), dma((4,)), dma((2, 2, PIECE_CHUNKS)),
                regular((4,)), regular, regular, regular, regular, regular, regular,
            ],
            compiler_params=pltpu.CompilerParams(collective_id=0, has_side_effects=True,
                                                 vmem_limit_bytes=62 * 1024 * 1024),
            cost_estimate=pl.CostEstimate(flops=2 * n_rows * n_cols * vecs * SWEEPS,
                                          bytes_accessed=n_rows * n_cols * 2 * PHASES, transcendentals=0),
        )(mat, x0, v_piece, weight, m0)
        return out

    vec = P(('col', 'row'), None)
    return jax.shard_map(step, mesh=mesh, in_specs=(P('row', 'col'), vec, vec, P(('col', 'row'))),
                         out_specs=vec, check_vma=False)
```

time: 3340 us -> 1430 us (0.43); the launches traced: 3300 us -> 1430 us
  waiting for transfers between devices: 1780 us -> 0 us
  Pallas kernels: 0 us -> 1400 us
  matrix products: 721 us -> 0 us
  blocking collectives: 694 us -> 10.2 us
  other arithmetic: 63.5 us -> 7.48 us
    pallas_call x0 -> x1, Pallas kernels: none -> 1400 us  [step(): pl.pallas_call(kernel, out_shape=[jax.ShapeDtypeStruct((piece, vecs), f32...]
    reduce_scatter x8 -> x0, waiting for transfers between devices: 1140 us -> none  [local_sweeps(): folded = lax.psum_scatter(part_prod, 'col', scatter_dimension=0, tiled=True)]
    dot_general x8 -> x0, matrix products: 721 us -> none  [local_sweeps(): part_prod = jnp.dot(mat_tile, x_src, preferred_element_type=jnp.float32)]
    psum x8 -> x0, blocking collectives: 694 us -> none  [local_sweeps(): lax.psum(jnp.sum(dang_col * x_cur, axis=0), ('col', 'row')) / vertex_count]
    all_gather x8 -> x0, waiting for transfers between devices: 646 us -> none  [local_sweeps(): lax.all_gather(x_cur.astype(jnp.bfloat16), 'row', axis=0, tiled=True)]
    convert_element_type x8 -> x1, other arithmetic: 47.9 us -> 0.71 us  [step(): dang_f = dang_piece.astype(jnp.float32)]
  transfers between devices with their start and end apart: 24 -> 0, of which waited for: 16 -> 0; matrix products, arithmetic and copies ran while one was open for 0% -> 0% of each run, Pallas kernels for 0% -> 0%
where the time goes in v2:
time: 1430 us
  Pallas kernels  1400 us (98%)
    pallas_call x1, Pallas kernels, step(): pl.pallas_call(kernel, out_shape=[jax.ShapeDtypeStruct((piece, vecs), f32...  1400 us

profile of v2, /device:TPU:3, one launch (start us, length us, event | category | flops | bytes accessed | tf_op | source)
XLA Modules:
  0.0 1426.6 jit_solution(18060118253680738282)
XLA Ops:
  0.0 0.7 convert_element_type.4
  0.7 0.0 copy-start
  0.7 3.8 bitcast_reduce_fusion
  4.5 0.6 pad_maximum_fusion.2.m0_ref
  5.1 10.2 all_gather.3
  15.4 0.0 copy-done
  15.4 0.4 convert.8
  15.8 0.2 slice_bitcast_fusion.1
  16.0 1.9 pad_maximum_fusion.x0_ref
  18.0 3.7 broadcast_in_dim.2.w_ref
  21.7 1398.7 %shard_map.46 = (f32[3072,512]{1,0:T(8,128)}, f32[2,6144,256]{2,1,0:T(8,128)}) custom-call(bf16[6144,12288]{1,0:T(8,128)(2,1)} %a_ref.1, bf16[2,3072,256]{2,1,0:T(8,128)(2,1)} %pad_maximum_fusion.x0_ref, f32[3072,512]{1,0:T(8,128)} %v_ref.1, f32[2,6144,128]{2,1,0:T(8,128)} %broadcast_in_dim.2.w_ref, f32[2,8,256]{2,1,0:T(8,128)} %pad_maximum_fusion.2.m0_ref), custom_call_target="tpu_custom_call" | custom-call | flops 618475290624 | bytes 2415919104 | tf_op jit(solution)/shard_map/pallas_call | solution.py:579
  1420.4 6.2 copy.6
  (3 shorter events, 0.1 us)
Async XLA Ops:
  0.7 14.7 %copy-start = (f32[3072,512]{1,0:T(8,128)S(1)}, f32[3072,512]{1,0:T(8,128)}, u32[]{:S(2)}) copy-start(f32[3072,512]{1,0:T(8,128)} %param.5) | copy-start | bytes 18874372

commit v3 on v2

--- a/solution.py
+++ b/solution.py
@@ -13,7 +13,6 @@
 GROUPS = 3
 CHUNKS = 4 * GROUPS
 PIECE_CHUNKS = CHUNKS // 2
-KSTEPS = 6
 UNITS = (7, 9, 7, 9)
 FIRST_FINAL = PHASES - HALVES
 LIVE_GROUPS = FIRST_FINAL * GROUPS
@@ -29,10 +28,10 @@
     pl.semaphore_signal(sem, inc=1, device_id={"col": dev[0], "row": dev[1]}, device_id_type=MESH)
 
 
-def kernel(a_ref, x0_ref, v_ref, w_ref, m0_ref, out_ref, vt_ref,
+def kernel(a_ref, x0_ref, v_ref, w_ref, m0_ref, fin_ref, vt_ref, cvec,
            xs, abuf, acc, part0, part1, part2, part3, recv0, recv1, recv3, side_in, cross_in, bst, round_in,
-           vbuf, wbuf, mrecv, cvec, fin,
-           a_sem, v_sem, w_sem, o_sem,
+           vbuf, wbuf, mrecv,
+           a_sem, v_sem, w_sem,
            fs, fr, side_r, cross_s, cross_r, bs, round_r, round_s, yrecv, xsend, xrecv, csend, crecv,
            gx_s, gx_r, gc_s, gc_r, gl_s, gl_r, g_loc, vs, vr,
            ms, mr, fin_r, cred_f, cred_side, cred_cross, cred_round, cred_c, cred_x, cred_y):
@@ -50,7 +49,6 @@
     size = tuple(u * unit for u in UNITS)
     start = (0, size[0], size[0] + size[1], size[0] + size[1] + size[2])
     span = sum(size)
-    depth = n_cols // KSTEPS
     piece = n_rows // 2
     width = x0_ref.shape[2]
     own_base = core * n_rows
@@ -61,24 +59,22 @@
         d = lax.rem(me + k, 8)
         return (d // 4, lax.rem(d, 4))
 
+    def tile_rows(gq, p):
+        return pl.ds(pl.multiple_of(gq * span + start[p], unit), size[p])
+
+    def half_cols(h):
+        return pl.ds(pl.multiple_of(h * width, width), width)
+
+    def a_copy(gq, p):
+        return pltpu.make_async_copy(a_ref.at[tile_rows(gq, p), :], abuf.at[p % 2, pl.ds(0, size[p])], a_sem.at[p % 2])
+
+    for p in range(2):
+        a_copy(0, p).start()
+
     barrier = pltpu.get_barrier_semaphore()
     for k in range(1, 8):
         signal(barrier, every_other(k))
     pl.semaphore_wait(barrier, 7)
-
-    def tile_rows(gq, p):
-        return pl.ds(pl.multiple_of(gq * span + start[p], unit), size[p])
-
-    def half_cols(h):
-        return pl.ds(pl.multiple_of(h * width, width), width)
-
-    def a_copy(gq, p, kb):
-        return pltpu.make_async_copy(
-            a_ref.at[tile_rows(gq, p), pl.ds(pl.multiple_of(kb * depth, depth), depth)],
-            abuf.at[kb, pl.ds(0, size[p])], a_sem.at[kb])
-
-    for kb in range(KSTEPS):
-        a_copy(0, 0, kb).start()
 
     def x_rows(h, r):
         return xs.at[h, pl.ds(pl.multiple_of(r * piece, piece), piece), :]
@@ -307,34 +303,27 @@
     def final_send(g, p):
         f, m, rows, owner = final_place(g, p)
         slot = lax.rem(g, 2)
-        return rcopy(parts[p].at[slot], fin.at[f, role, rows], fs.at[p, slot], fin_r.at[f, role, m], owner)
+        return rcopy(parts[p].at[slot], fin_ref.at[f, role, rows], fs.at[p, slot], fin_r.at[f, role, m], owner)
 
     def final_local(g, p):
         owner = final_place(g, p)[3]
         return jnp.logical_and(owner[0] == col, owner[1] == row)
 
-    def fin_rows(j, k):
-        return pl.ds(pl.multiple_of(j * (size[0] + size[1]) + k * size[0], unit), size[k])
-
-    def out_copy(f, j, k):
-        return pltpu.make_async_copy(fin.at[f, 0, fin_rows(j, k)],
-                                     out_ref.at[fin_rows(j, k), half_cols(f)], o_sem)
+    def final_keep(g, p):
+        f, m, rows, owner = final_place(g, p)
+        slot = lax.rem(g, 2)
+        return pltpu.make_async_copy(parts[p].at[slot], fin_ref.at[f, 0, rows], fs.at[p, slot])
+
+    def final_wait(g, p):
+        @pl.when(final_local(g, p))
+        def _():
+            final_keep(g, p).wait()
+
+        @pl.when(jnp.logical_not(final_local(g, p)))
+        def _():
+            final_send(g, p).wait_send()
 
     own_tile = 2 * col + row // 2 == row
-
-    def final_reduce(f, j, k):
-        rows = fin_rows(j, k)
-        tele = pltpu.make_async_copy(v_ref.at[rows, half_cols(f)], vbuf.at[pl.ds(0, size[k])], v_sem)
-        tele.start()
-        for r in range(2):
-            skip = jnp.logical_and(own_tile, home) if r == 0 else jnp.bool_(False)
-
-            @pl.when(jnp.logical_not(skip))
-            def _():
-                rcopy(fin.at[f, r, rows], fin.at[f, r, rows], fs.at[0, 0], fin_r.at[f, r, 2 * j + k], cdev).wait_recv()
-        tele.wait()
-        fin[f, 0, rows] = (fin[f, 0, rows] + fin[f, 1, rows]) + cvec[f] * vbuf[0:size[k]]
-        out_copy(f, j, k).start()
 
     def substep(g, p):
         q, gq = lax.div(g, GROUPS), lax.rem(g, GROUPS)
@@ -379,22 +368,13 @@
             def _():
                 w_copy(1, g - 2, 2).start()
 
-        acc[0:rows] = jnp.zeros((rows, width), jnp.float32)
-        nxt_p = (p + 1) % 4
-        nxt_gq = lax.rem(gq + 1, GROUPS) if p == 3 else gq
-        more = g < TOTAL_GROUPS - 1 if p == 3 else jnp.bool_(True)
-
-        def kstep(kb, carry):
-            a_copy(gq, p, kb).wait()
-            acc[0:rows] += jnp.dot(abuf[kb, 0:rows], xs[b, pl.ds(pl.multiple_of(kb * depth, depth), depth), :],
-                                   preferred_element_type=jnp.float32)
-
-            @pl.when(more)
-            def _():
-                a_copy(nxt_gq, nxt_p, kb).start()
-            return carry
-
-        lax.fori_loop(0, KSTEPS, kstep, 0)
+        a_copy(gq, p).wait()
+        acc[0:rows] = jnp.dot(abuf[p % 2, 0:rows], xs[b], preferred_element_type=jnp.float32)
+        later_gq = lax.rem(gq + 1, GROUPS) if p >= 2 else gq
+
+        @pl.when(g < TOTAL_GROUPS - 1 if p >= 2 else jnp.bool_(True))
+        def _():
+            a_copy(later_gq, (p + 2) % 4).start()
 
         if p == 3:
             @pl.when(jnp.logical_and(gq == GROUPS - 1, q < FIRST_FINAL - 1))
@@ -414,9 +394,7 @@
 
         @pl.when(g - 2 >= LIVE_GROUPS)
         def _():
-            @pl.when(jnp.logical_not(final_local(g - 2, p)))
-            def _():
-                final_send(g - 2, p).wait_send()
+            final_wait(g - 2, p)
 
         @pl.when(is_live)
         def _():
@@ -446,15 +424,14 @@
 
         @pl.when(jnp.logical_not(is_live))
         def _():
-            f, m, at, owner = final_place(g, p)
+            parts[p][slot] = DAMPING * acc[0:rows]
 
             @pl.when(final_local(g, p))
             def _():
-                fin[f, 0, at] = DAMPING * acc[0:rows]
+                final_keep(g, p).start()
 
             @pl.when(jnp.logical_not(final_local(g, p)))
             def _():
-                parts[p][slot] = DAMPING * acc[0:rows]
                 final_send(g, p).start()
 
         if p == 0:
@@ -523,18 +500,19 @@
 
     lax.fori_loop(0, TOTAL_GROUPS, group, 0)
 
-    for f in range(HALVES):
-        def body(j, carry):
-            final_reduce(f, j, 0)
-            final_reduce(f, j, 1)
-            return carry
-        lax.fori_loop(0, PIECE_CHUNKS // 2, body, 0)
-
     for g in (TOTAL_GROUPS - 2, TOTAL_GROUPS - 1):
         for p in range(4):
-            @pl.when(jnp.logical_not(final_local(jnp.int32(g), p)))
-            def _():
-                final_send(jnp.int32(g), p).wait_send()
+            final_wait(jnp.int32(g), p)
+
+    for f in range(HALVES):
+        for r in range(2):
+            skip = jnp.logical_and(own_tile, home) if r == 0 else jnp.bool_(False)
+
+            @pl.when(jnp.logical_not(skip))
+            def _():
+                for m in range(PIECE_CHUNKS):
+                    got = fin_ref.at[f, r, pl.ds(piece_start(m), size[m % 2])]
+                    rcopy(got, got, fs.at[0, 0], fin_r.at[f, r, m], cdev).wait_recv()
 
     @pl.when(far)
     def _():
@@ -547,11 +525,21 @@
             for m in range(PIECE_CHUNKS):
                 tele_send(h, m).wait_send()
 
-    def drain(j, carry):
-        out_copy(0, 0, 0).wait()
-        out_copy(0, 0, 1).wait()
-        return carry
-    lax.fori_loop(0, HALVES * PIECE_CHUNKS // 2, drain, 0)
+
+def dang_kernel(d_ref, all_ref, send_sem, recv_sem):
+    me = lax.axis_index("col") * 4 + lax.axis_index("row")
+    barrier = pltpu.get_barrier_semaphore()
+    others = [lax.rem(me + k, 8) for k in range(1, 8)]
+    for d in others:
+        signal(barrier, (d // 4, lax.rem(d, 4)))
+    pl.semaphore_wait(barrier, 7)
+    for d in others:
+        rcopy(d_ref, all_ref.at[me], send_sem, recv_sem, (d // 4, lax.rem(d, 4))).start()
+    all_ref[me] = d_ref[...]
+    seven = all_ref.at[pl.ds(0, 7)]
+    whole = rcopy(seven, seven, send_sem, recv_sem, (0, 0))
+    whole.wait_recv()
+    whole.wait_send()
 
 
 def solution(mesh):
@@ -560,12 +548,19 @@
         n_rows, n_cols = mat.shape
         piece, vecs = x_piece.shape
         width = vecs // HALVES
-        unit, depth = n_rows // 96, n_cols // KSTEPS
+        unit = n_rows // 96
         small, large = UNITS[0] * unit, UNITS[1] * unit
         lanes = min(128, width)
 
         dang_f = dang_piece.astype(jnp.float32)
-        dang_all = lax.all_gather(dang_f, ('col', 'row'), axis=0, tiled=True)
+        dang_all = pl.pallas_call(
+            dang_kernel,
+            out_shape=jax.ShapeDtypeStruct((8, piece // 128, 128), jnp.float32),
+            in_specs=[pl.BlockSpec(memory_space=pltpu.VMEM)],
+            out_specs=pl.BlockSpec(memory_space=pltpu.VMEM),
+            scratch_shapes=[pltpu.SemaphoreType.DMA, pltpu.SemaphoreType.DMA],
+            compiler_params=pltpu.CompilerParams(collective_id=1, has_side_effects=True),
+        )(dang_f.reshape(piece // 128, 128)).reshape(-1)
         tiles = jnp.stack([lax.dynamic_slice(dang_all, (i * n_rows,), (n_rows,)),
                            lax.dynamic_slice(dang_all, (lax.rem(i + 2, 4) * n_rows,), (n_rows,))])
         weight = jnp.broadcast_to(tiles[:, :, None], (2, n_rows, lanes))
@@ -576,15 +571,16 @@
         f32, bf16 = jnp.float32, jnp.bfloat16
         dma, regular = pltpu.SemaphoreType.DMA, pltpu.SemaphoreType.REGULAR
         hbm = pl.BlockSpec(memory_space=pl.ANY)
-        out, _ = pl.pallas_call(
+        fin, _, scale = pl.pallas_call(
             kernel,
-            out_shape=[jax.ShapeDtypeStruct((piece, vecs), f32),
-                       jax.ShapeDtypeStruct((HALVES, n_rows, width), f32)],
+            out_shape=[jax.ShapeDtypeStruct((HALVES, 2, piece, width), f32),
+                       jax.ShapeDtypeStruct((HALVES, n_rows, width), f32),
+                       jax.ShapeDtypeStruct((HALVES, 1, width), f32)],
             in_specs=[hbm, hbm, hbm, hbm, pl.BlockSpec(memory_space=pltpu.VMEM)],
-            out_specs=[hbm, hbm],
+            out_specs=[hbm, hbm, pl.BlockSpec(memory_space=pltpu.VMEM)],
             scratch_shapes=[
                 pltpu.VMEM((3, n_cols, width), bf16),
-                pltpu.VMEM((KSTEPS, large, depth), bf16),
+                pltpu.VMEM((2, large, n_cols), bf16),
                 pltpu.VMEM((large, width), f32),
                 pltpu.VMEM((2, small, width), f32),
                 pltpu.VMEM((2, large, width), f32),
@@ -600,9 +596,7 @@
                 pltpu.VMEM((large, width), f32),
                 pltpu.VMEM((large, lanes), f32),
                 pltpu.VMEM((4, 8, 8, width), f32),
-                pltpu.VMEM((2, 1, width), f32),
-                pltpu.VMEM((2, 2, piece, width), f32),
-                dma((KSTEPS,)), dma, dma, dma,
+                dma((2,)), dma, dma,
                 dma((4, 2)), dma((4, 2)),
                 dma((3,)), dma, dma((2,)),
                 dma((2,)), dma((4,)), dma, dma((2, GROUPS)),
@@ -617,7 +611,8 @@
             cost_estimate=pl.CostEstimate(flops=2 * n_rows * n_cols * vecs * SWEEPS,
                                           bytes_accessed=n_rows * n_cols * 2 * PHASES, transcendentals=0),
         )(mat, x0, v_piece, weight, m0)
-        return out
+        halves = [(fin[h, 0] + fin[h, 1]) + scale[h] * v_piece[:, h * width:(h + 1) * width] for h in range(HALVES)]
+        return jnp.concatenate(halves, axis=1)
 
     vec = P(('col', 'row'), None)
     return jax.shard_map(step, mesh=mesh, in_specs=(P('row', 'col'), vec, vec, P(('col', 'row'))),

time: 1430 us -> 1480 us (1.035)
  Pallas kernels: 1400 us -> 1450 us
    pallas_call x1 -> x2, Pallas kernels: 1400 us -> 1450 us  [the longest x1 1440 us: step(): pl.pallas_call(kernel, out_shape=[jax.ShapeDtypeStruct((HALVES, 2, piece,...]
where the time goes in v3:
time: 1480 us
  Pallas kernels  1450 us (98%)
  other arithmetic  21.3 us (1%)
    pallas_call x1, Pallas kernels, step(): pl.pallas_call(kernel, out_shape=[jax.ShapeDtypeStruct((HALVES, 2, piece,...  1440 us

profile of v3, /device:TPU:3, one launch (start us, length us, event | category | flops | bytes accessed | tf_op | source)
XLA Modules:
  0.0 1478.0 jit_solution(7641819673083551301)
XLA Ops:
  0.0 1.3 fusion.1
  1.3 3.5 bitcast_reduce_fusion
  4.8 0.6 pad_maximum_fusion.3.m0_ref
  5.4 6.6 shard_map.46
  12.0 0.8 fusion
  12.8 3.2 convert.8
  16.0 0.2 slice_bitcast_fusion.1
  16.2 2.0 pad_maximum_fusion.1.x0_ref
  18.2 3.7 broadcast_in_dim.2.w_ref
  22.0 1444.7 %shard_map.47 = (f32[2,2,3072,256]{3,2,1,0:T(8,128)}, f32[2,6144,256]{2,1,0:T(8,128)}, f32[2,1,256]{2,1,0:T(1,128)}) custom-call(bf16[6144,12288]{1,0:T(8,128)(2,1)} %a_ref.1, bf16[2,3072,256]{2,1,0:T(8,128)(2,1)} %pad_maximum_fusion.1.x0_ref, f32[3072,512]{1,0:T(8,128)} %v_ref.1, f32[2,6144,128]{2,1,0:T(8,128)} %broadcast_in_dim.2.w_ref, ...), custom_call_target="tpu_custom_call" | custom-call | flops 618475290624 | bytes 2415919104 | tf_op jit(solution)/shard_map/pallas_call | solution.py:574
  1466.7 0.6 fusion.2
  1467.4 7.0 bitcast_add_fusion.1
  1474.3 3.7 pad_maximum_fusion
  (2 shorter events, 0.1 us)

commit v4 on v3

--- a/solution.py
+++ b/solution.py
@@ -13,6 +13,7 @@
 GROUPS = 3
 CHUNKS = 4 * GROUPS
 PIECE_CHUNKS = CHUNKS // 2
+KSTEPS = 3
 UNITS = (7, 9, 7, 9)
 FIRST_FINAL = PHASES - HALVES
 LIVE_GROUPS = FIRST_FINAL * GROUPS
@@ -65,11 +66,16 @@
     def half_cols(h):
         return pl.ds(pl.multiple_of(h * width, width), width)
 
-    def a_copy(gq, p):
-        return pltpu.make_async_copy(a_ref.at[tile_rows(gq, p), :], abuf.at[p % 2, pl.ds(0, size[p])], a_sem.at[p % 2])
+    depth = n_cols // KSTEPS
+
+    def a_copy(gq, p, kb):
+        return pltpu.make_async_copy(
+            a_ref.at[tile_rows(gq, p), pl.ds(pl.multiple_of(kb * depth, depth), depth)],
+            abuf.at[p % 2, kb, pl.ds(0, size[p])], a_sem.at[p % 2, kb])
 
     for p in range(2):
-        a_copy(0, p).start()
+        for kb in range(KSTEPS):
+            a_copy(0, p, kb).start()
 
     barrier = pltpu.get_barrier_semaphore()
     for k in range(1, 8):
@@ -368,13 +374,21 @@
             def _():
                 w_copy(1, g - 2, 2).start()
 
-        a_copy(gq, p).wait()
-        acc[0:rows] = jnp.dot(abuf[p % 2, 0:rows], xs[b], preferred_element_type=jnp.float32)
         later_gq = lax.rem(gq + 1, GROUPS) if p >= 2 else gq
-
-        @pl.when(g < TOTAL_GROUPS - 1 if p >= 2 else jnp.bool_(True))
-        def _():
-            a_copy(later_gq, (p + 2) % 4).start()
+        more = g < TOTAL_GROUPS - 1 if p >= 2 else jnp.bool_(True)
+        acc[0:rows] = jnp.zeros((rows, width), jnp.float32)
+
+        def kstep(kb, carry):
+            a_copy(gq, p, kb).wait()
+            acc[0:rows] += jnp.dot(abuf[p % 2, kb, 0:rows], xs[b, pl.ds(pl.multiple_of(kb * depth, depth), depth), :],
+                                   preferred_element_type=jnp.float32)
+
+            @pl.when(more)
+            def _():
+                a_copy(later_gq, (p + 2) % 4, kb).start()
+            return carry
+
+        lax.fori_loop(0, KSTEPS, kstep, 0)
 
         if p == 3:
             @pl.when(jnp.logical_and(gq == GROUPS - 1, q < FIRST_FINAL - 1))
@@ -580,7 +594,7 @@
             out_specs=[hbm, hbm, pl.BlockSpec(memory_space=pltpu.VMEM)],
             scratch_shapes=[
                 pltpu.VMEM((3, n_cols, width), bf16),
-                pltpu.VMEM((2, large, n_cols), bf16),
+                pltpu.VMEM((2, KSTEPS, large, n_cols // KSTEPS), bf16),
                 pltpu.VMEM((large, width), f32),
                 pltpu.VMEM((2, small, width), f32),
                 pltpu.VMEM((2, large, width), f32),
@@ -596,7 +610,7 @@
                 pltpu.VMEM((large, width), f32),
                 pltpu.VMEM((large, lanes), f32),
                 pltpu.VMEM((4, 8, 8, width), f32),
-                dma((2,)), dma, dma,
+                dma((2, KSTEPS)), dma, dma,
                 dma((4, 2)), dma((4, 2)),
                 dma((3,)), dma, dma((2,)),
                 dma((2,)), dma((4,)), dma, dma((2, GROUPS)),

time: 1480 us -> 1430 us (0.966)
  Pallas kernels: 1450 us -> 1400 us
    pallas_call x1, Pallas kernels: 1440 us -> 1390 us  [step(): pl.pallas_call(kernel, out_shape=[jax.ShapeDtypeStruct((HALVES, 2, piece,...]
where the time goes in v4:
time: 1430 us
  Pallas kernels  1400 us (98%)
  other arithmetic  21.3 us (1%)
    pallas_call x1, Pallas kernels, step(): pl.pallas_call(kernel, out_shape=[jax.ShapeDtypeStruct((HALVES, 2, piece,...  1390 us

profile of v4, /device:TPU:3, one launch (start us, length us, event | category | flops | bytes accessed | tf_op | source)
XLA Modules:
  0.0 1427.6 jit_solution(12889123893357931779)
XLA Ops:
  0.0 1.3 fusion.1
  1.3 3.5 bitcast_reduce_fusion
  4.8 0.6 pad_maximum_fusion.3.m0_ref
  5.4 6.6 shard_map.46
  12.0 0.8 fusion
  12.8 3.2 convert.8
  16.0 0.2 slice_bitcast_fusion.1
  16.2 2.0 pad_maximum_fusion.1.x0_ref
  18.2 3.7 broadcast_in_dim.2.w_ref
  22.0 1394.3 %shard_map.47 = (f32[2,2,3072,256]{3,2,1,0:T(8,128)}, f32[2,6144,256]{2,1,0:T(8,128)}, f32[2,1,256]{2,1,0:T(1,128)}) custom-call(bf16[6144,12288]{1,0:T(8,128)(2,1)} %a_ref.1, bf16[2,3072,256]{2,1,0:T(8,128)(2,1)} %pad_maximum_fusion.1.x0_ref, f32[3072,512]{1,0:T(8,128)} %v_ref.1, f32[2,6144,128]{2,1,0:T(8,128)} %broadcast_in_dim.2.w_ref, ...), custom_call_target="tpu_custom_call" | custom-call | flops 618475290624 | bytes 2415919104 | tf_op jit(solution)/shard_map/pallas_call | solution.py:588
  1416.3 0.6 fusion.2
  1416.9 7.0 bitcast_add_fusion.1
  1423.9 3.7 pad_maximum_fusion
  (2 shorter events, 0.1 us)
